TPU v7x, 128 devices: a whole 4x4x4 slice. The times are simulated.
128 devices in a mesh: dp: 16 (over y, z), vocab: 8 (over x, core).
Axes of the slice: x: 4, y: 4, z: 4, core: 2. Of those that a mesh axis runs over, the one named last changes fastest.
Arguments:
- tokens: bfloat16 [2048, 7168], P('dp'), may hold values from -6 to 6
- expert_hidden: bfloat16 [2048, 8, 1024], P('dp'), may hold values from -6 to 6
- routes: int32 [2048, 8], P('dp'), may hold values from 0 to 63, all different within a row; in each aligned block of 16 rows (0 to 15, 16 to 31, ...) at most 3 rows name the same one
- route_weight: float32 [2048, 8], P('dp'), may hold values from 0.05 to 0.45
- expert_weight: bfloat16 [128, 512, 7168], P(('dp', 'vocab')), may hold values from -0.1875 to 0.1875
- norm_gain: float32 [7168], replicated, may hold values from 0.5 to 1.5
- head_weight: bfloat16 [7168, 114688], P(None, ('dp', 'vocab')), may hold values from -8 to 8
- targets: int32 [2048], P('dp'), may hold values from 0 to 114687
- rollout_logprob: float32 [2048], P('dp'), may hold values from -21 to -13
- advantages: float32 [2048], P('dp'), may hold values from -5 to 5
Outputs:
- layer_out: bfloat16 [2048, 7168], P('dp')
- token_logprob: float32 [2048], P('dp')
- token_loss: float32 [2048], P('dp')
Inputs may be any that keep to these rules, and one draw needn't show every extreme that they name: The 8 routes of a token name different experts; among the routes of one aligned block of 16 token rows, no expert is named more than 3 times.
All inputs are finite; a program needn't handle non-finite values.
Results may differ from a plain program's by a relative error of at most 0.02.
Values may be sent and summed in bfloat16 or wider, within the bound.
No kernel may reach another device: no remote copies, remote signals or barrier semaphores. Data moves between devices by JAX's collectives and lax.ppermute only.
A program may use at most 192 MiB of HBM per device.

v0:
```python
import jax
import jax.numpy as jnp
from jax import lax
from jax.sharding import Mesh
from jax.sharding import PartitionSpec as P

X = "vocab_0"
CORE = "vocab_1"
VOCAB = ("vocab_0", "vocab_1")
DP_VOCAB = ("dp_0", "dp_1", "vocab_0", "vocab_1")
DP = ("dp_0", "dp_1")
norm_epsilon = 1e-06
clip_low = 0.8
clip_high = 1.2
dual_bound = 3.0
bf16 = jnp.bfloat16
f32 = jnp.float32


def clipped_loss(logprob, rollout_logprob, advantages):
    ratio = jnp.exp(logprob - rollout_logprob)
    surrogate = jnp.minimum(ratio * advantages, jnp.clip(ratio, clip_low, clip_high) * advantages)
    bounded = jnp.where(
        advantages < 0.0, jnp.maximum(surrogate, dual_bound * advantages), surrogate
    )
    return -bounded


def dot(a, b):
    return jnp.dot(a, b, preferred_element_type=f32)


def swap_cores(x):
    return lax.ppermute(x, CORE, [(0, 1), (1, 0)])


def label_row(targets):
    digits = [targets // 128**k % 128 for k in range(3)]
    row = jnp.concatenate(digits + [jnp.zeros_like(targets)]).astype(bf16)
    return row[None]


def labels_of(rows):
    digits = rows.astype(f32).astype(jnp.int32).reshape(rows.shape[0], 4, 128)
    return digits[:, 0] + 128 * digits[:, 1] + 128 * 128 * digits[:, 2]


def experts_stage(tokens, expert_hidden, routes, route_weight, expert_weight, targets):
    x, h = (lax.axis_index(X), lax.axis_index(CORE))
    rows, top = routes.shape
    width = expert_hidden.shape[2] // 2
    cols = tokens.shape[1] // 2
    blocks = rows // 16
    by_block = routes.reshape(blocks, 16 * top).T
    mine = (by_block[:, :, None] == (lax.iota(jnp.int32, 16) * 4 + x)[None, None, :]).astype(bf16)
    n = 16 * top
    lower = (lax.iota(jnp.int32, n)[:, None] > lax.iota(jnp.int32, n)[None, :]).astype(bf16)
    before = dot(lower, mine.reshape(n, blocks * 16)).reshape(n, blocks, 16)
    slot = jnp.sum(before * mine.astype(f32), axis=2).astype(jnp.int32)
    place = by_block // 4 * 24 + lax.iota(jnp.int32, blocks)[None, :] * 3 + slot
    place = jnp.where(by_block % 4 == x, place, -1).T.reshape(rows, top)
    select = (lax.iota(jnp.int32, 384)[:, None] == place.reshape(-1)[None, :]).astype(bf16)
    hidden = lax.dynamic_slice_in_dim(
        expert_hidden.reshape(rows * top, 2 * width), h * width, width, 1
    )
    buffer = dot(select, hidden).astype(bf16).reshape(16, 24, width)
    extra = jnp.pad(label_row(targets), ((0, 7), (0, 0)))
    buffer = jnp.concatenate([buffer, jnp.broadcast_to(extra[None], (16, 8, width))], axis=1)
    received = lax.all_to_all(buffer, DP, 0, 0, tiled=True)
    labels = labels_of(received[:, 24])
    own = received[:, :24].reshape(384, width)
    other = swap_cores(own)
    weight = expert_weight[0]
    weight_own = lax.dynamic_slice_in_dim(weight, h * cols, cols, 1)
    weight_other = swap_cores(lax.dynamic_slice_in_dim(weight, (1 - h) * cols, cols, 1))
    product = (dot(own, weight_own) + dot(other, weight_other)).astype(bf16)
    back = lax.all_to_all(product.reshape(16, 24, cols), DP, 0, 0, tiled=True)
    gate = jnp.sum(
        jnp.where(
            place[:, :, None] == lax.iota(jnp.int32, 384)[None, None, :],
            route_weight[:, :, None],
            0.0,
        ),
        axis=1,
    )
    gate_high = gate.astype(bf16)
    gate_low = (gate - gate_high.astype(f32)).astype(bf16)
    both = dot(jnp.concatenate([gate_high, gate_low]), back.reshape(384, cols))
    partial = (both[:rows] + both[rows:]).astype(bf16)
    parts = lax.all_to_all(partial.reshape(4, rows // 4, cols), X, 0, 0, tiled=True)
    moe = jnp.sum(parts.astype(f32), axis=0)
    mine_tokens = lax.dynamic_slice(tokens, (x * (rows // 4), h * cols), (rows // 4, cols))
    return ((mine_tokens.astype(f32) + moe).astype(bf16), labels)


def combined(peaks, totals, picks):
    peak = jnp.max(peaks, axis=0)
    return (peak, jnp.sum(totals * jnp.exp(peaks - peak), axis=0), jnp.sum(picks, axis=0))


def per_device(
    tokens,
    expert_hidden,
    routes,
    route_weight,
    expert_weight,
    norm_gain,
    head_weight,
    targets,
    rollout_logprob,
    advantages,
):
    h = lax.axis_index(CORE)
    tile, labels = experts_stage(
        tokens, expert_hidden, routes, route_weight, expert_weight, targets
    )
    sub, cols = (tile.shape[0] // 2, tile.shape[1])
    kept = lax.dynamic_slice_in_dim(tile, h * sub, sub, 0)
    got = swap_cores(lax.dynamic_slice_in_dim(tile, (1 - h) * sub, sub, 0))
    layer_sub = jnp.where(
        h == 0, jnp.concatenate([kept, got], axis=1), jnp.concatenate([got, kept], axis=1)
    )
    group_layer = lax.all_to_all(
        jnp.broadcast_to(layer_sub[None], (8, *layer_sub.shape)), VOCAB, 0, 0, tiled=True
    ).reshape(tokens.shape)
    widened = layer_sub.astype(f32)
    mean_square = jnp.mean(widened * widened, axis=-1, keepdims=True)
    normed_sub = (widened * lax.rsqrt(mean_square + norm_epsilon) * norm_gain).astype(bf16)
    voc_dev = head_weight.shape[1]
    columns = lax.axis_index(DP_VOCAB) * voc_dev + lax.iota(jnp.int32, voc_dev)
    by_device = labels.reshape(-1, 2, sub // 2)
    stats = []
    for c in range(2):
        piece = normed_sub[c * (sub // 2) : (c + 1) * (sub // 2)]
        normed = lax.all_gather(piece, DP_VOCAB, axis=0, tiled=True)
        logits = dot(normed, head_weight)
        peak = jnp.max(logits, axis=1)
        total = jnp.sum(jnp.exp(logits - peak[:, None]), axis=1)
        wanted = by_device[:, c].reshape(-1)
        picked = jnp.sum(jnp.where(columns[None, :] == wanted[:, None], logits, 0.0), axis=1)
        stats.append(jnp.stack([peak, total, picked]).reshape(3, -1, 1, sub // 2))
    stats = jnp.concatenate(stats, axis=2).reshape(3, 16, -1).transpose(1, 0, 2)
    sent = lax.all_to_all(stats, DP, 0, 0, tiled=True)
    group = jnp.stack(combined(sent[:, 0], sent[:, 1], sent[:, 2]))
    sent = lax.all_gather(group, VOCAB, axis=0)
    peak, total, target_logit = combined(sent[:, 0], sent[:, 1], sent[:, 2])
    token_logprob = target_logit - (peak + jnp.log(total))
    token_loss = clipped_loss(token_logprob, rollout_logprob, advantages)
    return (group_layer, token_logprob, token_loss)


def solution(mesh):
    torus = Mesh(mesh.devices.reshape(4, 4, 4, 2), ("dp_0", "dp_1", "vocab_0", "vocab_1"))
    placed = (
        P(DP, None),
        P(DP, None, None),
        P(DP, None),
        P(DP, None),
        P(DP_VOCAB, None, None),
        P(),
        P(None, DP_VOCAB),
        P(DP),
        P(DP),
        P(DP),
    )
    return jax.shard_map(
        per_device,
        mesh=torus,
        in_specs=placed,
        out_specs=(P(DP, None), P(DP), P(DP)),
        check_vma=False,
    )
```

profile of v0, /device:TPU:1, one launch (start us, length us, event | category | flops | bytes accessed | tf_op | source)
XLA Modules:
  0.0 330.1 jit_solution(12316371568212583948)
XLA Ops:
  7.2 4.3 %dynamic-slice_bitcast_fusion = bf16[512,3584]{1,0:T(8,128)(2,1)} fusion(bf16[1,512,7168]{2,1,0:T(8,128)(2,1)} %param.14, s32[]{:T(128)S(6)} %select_n.101), kind=kLoop, calls=%fused_computation.8 | loop fusion | bytes 7340036 | tf_op jit(solution)/shard_map/dynamic_slice | solution.py:75
  11.5 1.4 collective-permute-start.1
  13.6 0.6 fusion.6
  14.2 17.8 %all_to_all.25 = bf16[16,32,512]{2,1,0:T(8,128)(2,1)S(1)} all-to-all(bf16[16,32,512]{2,1,0:T(8,128)(2,1)S(1)} %pad_maximum_fusion), channel_id=1, replica_groups=mesh['dp_0'=4,'dp_1'=4,'vocab_0'=4,'vocab_1'=2] {'dp_0','dp_1'}, dimensions={0} | all-to-all | bytes 1048576 | tf_op jit(solution)/shard_map/all_to_all | solution.py:69
  32.1 2.4 collective-permute-start
  34.5 3.6 %fusion.1 = f32[384,3584]{1,0:T(8,128)S(1)} fusion(bf16[384,512]{1,0:T(8,128)(2,1)S(1)} %bitcast.58, bf16[1,512,7168]{2,1,0:T(8,128)(2,1)} %param.14, s32[]{:T(128)S(6)} %select_n.90), kind=kOutput, calls=%fused_computation.2 | convolution fusion | flops 1409286144 | bytes 9568260 | tf_op jit(solution)/shard_map/dot_general | solution.py:30
  38.1 5.2 %fusion = bf16[384,3584]{1,0:T(8,128)(2,1)} fusion(f32[384,3584]{1,0:T(8,128)S(1)} %fusion.1, bf16[384,512]{1,0:T(8,128)(2,1)S(1)} %collective-permute-done, bf16[512,3584]{1,0:T(8,128)(2,1)} %collective-permute-done.1), kind=kOutput, calls=%fused_computation.1 | convolution fusion | flops 1412038656 | bytes 12320768 | tf_op jit(solution)/shard_map/dot_general | solution.py:30
  43.3 3.9 %all-to-all-start.1 = ((bf16[16,24,3584]{2,1,0:T(8,128)(2,1)}), bf16[16,24,3584]{2,1,0:T(8,128)(2,1)S(1)}, u32[]{:S(2)}, u32[]{:S(2)}) async-start(bf16[16,24,3584]{2,1,0:T(8,128)(2,1)} %bitcast.56), calls=%async_computation.1 | async-start | bytes 5505024 | tf_op jit(solution)/shard_map/all_to_all | solution.py:77
  47.4 0.5 select_reduce_fusion.2
  48.0 36.7 %all-to-all-done.1 = bf16[16,24,3584]{2,1,0:T(8,128)(2,1)S(1)} async-done(((bf16[16,24,3584]{2,1,0:T(8,128)(2,1)}), bf16[16,24,3584]{2,1,0:T(8,128)(2,1)S(1)}, u32[]{:S(2)}, u32[]{:S(2)}) %all-to-all-start.1) | async-done | bytes 2752544 | tf_op jit(solution)/shard_map/all_to_all | solution.py:77
  84.7 1.1 fusion.13
  85.8 1.1 fusion.4
  86.9 4.1 %all-to-all-start.2 = ((bf16[4,32,3584]{2,1,0:T(8,128)(2,1)}), bf16[4,32,3584]{2,1,0:T(8,128)(2,1)S(1)}, u32[]{:S(2)}, u32[]{:S(2)}) async-start(bf16[4,32,3584]{2,1,0:T(8,128)(2,1)} %bitcast.17), calls=%async_computation.2 | async-start | bytes 1835008 | tf_op jit(solution)/shard_map/all_to_all | solution.py:90
  91.0 12.0 %all-to-all-done.2 = bf16[4,32,3584]{2,1,0:T(8,128)(2,1)S(1)} async-done(((bf16[4,32,3584]{2,1,0:T(8,128)(2,1)}), bf16[4,32,3584]{2,1,0:T(8,128)(2,1)S(1)}, u32[]{:S(2)}, u32[]{:S(2)}) %all-to-all-start.2) | async-done | bytes 917536 | tf_op jit(solution)/shard_map/all_to_all | solution.py:90
  103.2 1.0 add_convert_fusion
  104.2 2.7 collective-permute-start.2
  106.9 1.0 collective-permute-done.2
  108.2 0.7 fusion.42
  109.0 0.7 all-gather.7.cloned.1.call-update
  110.6 1.4 broadcast_in_dim.25
  112.0 4.6 %all-to-all-start.3 = ((bf16[8,16,7168]{2,1,0:T(8,128)(2,1)}), bf16[8,16,7168]{2,1,0:T(8,128)(2,1)}, u32[]{:S(2)}, u32[]{:S(2)}) async-start(bf16[8,16,7168]{2,1,0:T(8,128)(2,1)} %broadcast_in_dim.25), calls=%async_computation.3 | async-start | bytes 3670016 | tf_op jit(solution)/shard_map/all_to_all | solution.py:123
  116.6 71.4 %all-gather.5.cloned.1.call-done = bf16[1024,7168]{1,0:T(8,128)(2,1)} async-done(((bf16[8,7168]{1,0:T(8,128)(2,1)}), bf16[1024,7168]{1,0:T(8,128)(2,1)}) %all-gather.5.cloned.1.call-update) | async-done | bytes 14680080 | tf_op jit(solution)/shard_map/all_gather | solution.py:135
  188.0 20.6 %fusion.44 = (f32[1024]{0:T(1024)S(1)}, f32[1024,896]{0,1:T(8,128)}) fusion(bf16[1024,7168]{1,0:T(8,128)(2,1)} %all-gather.5.cloned.1.call-done, bf16[7168,896]{1,0:T(8,128)(2,1)} %param.16), kind=kOutput, calls=%fused_computation.106 | convolution fusion | flops 13154253824 | bytes 31199232 | tf_op jit(solution)/shard_map/dot_general | solution.py:30
  208.7 58.5 %all-gather.7.cloned.1.call-done = bf16[1024,7168]{1,0:T(8,128)(2,1)} async-done(((bf16[8,7168]{1,0:T(8,128)(2,1)}), bf16[1024,7168]{1,0:T(8,128)(2,1)}) %all-gather.7.cloned.1.call-update) | async-done | bytes 14680080 | tf_op jit(solution)/shard_map/all_gather | solution.py:135
  267.2 20.9 %fusion.45 = (f32[1024]{0:T(1024)S(1)}, f32[1024,896]{0,1:T(8,128)}) fusion(bf16[1024,7168]{1,0:T(8,128)(2,1)} %all-gather.7.cloned.1.call-done, bf16[7168,896]{1,0:T(8,128)(2,1)} %param.16), kind=kOutput, calls=%fused_computation.107 | convolution fusion | flops 13154253824 | bytes 31199232 | tf_op jit(solution)/shard_map/dot_general | solution.py:30
  288.3 4.3 %exponential_reduce_fusion.1 = (f32[1024]{0:T(1024)S(1)}, f32[1024]{0:T(1024)S(1)}, f32[1024]{0:T(1024)S(1)}, f32[1024]{0:T(1024)S(1)}) fusion(f32[1024,896]{0,1:T(8,128)} %get-tuple-element.32, f32[1024]{0:T(1024)S(1)} %get-tuple-element.31, s32[1024]{0:T(1024)S(1)} %eq.118, s32[896]{0:T(1024)S(1)} %iota_add_fusion, f32[1024,896]{0,1:T(8,128)} %get-tuple-element.34, ...), kind=kLoop, calls=%fused_computation.7 | loop fusion | flops 9170944 | bytes 7376384 | tf_op jit(solution)/shard_map/reduce_sum | solution.py:138
  294.1 0.6 copy.49
  294.7 5.7 %all-to-all-start.4 = ((f32[16,3,128]{2,1,0:T(4,128)}), f32[16,3,128]{2,1,0:T(4,128)S(1)}, u32[]{:S(2)}, u32[]{:S(2)}) async-start(f32[16,3,128]{2,1,0:T(4,128)} %copy.49), calls=%async_computation.4 | async-start | bytes 65536 | tf_op jit(solution)/shard_map/all_to_all | solution.py:143
  300.5 6.5 %all-to-all-done.4 = f32[16,3,128]{2,1,0:T(4,128)S(1)} async-done(((f32[16,3,128]{2,1,0:T(4,128)}), f32[16,3,128]{2,1,0:T(4,128)S(1)}, u32[]{:S(2)}, u32[]{:S(2)}) %all-to-all-start.4) | async-done | bytes 24608 | tf_op jit(solution)/shard_map/all_to_all | solution.py:143
  307.0 12.8 %all-gather.1 = f32[8,3,128]{2,1,0:T(4,128)S(1)} all-gather(f32[1,3,128]{2,1,0:T(4,128)S(1)} %maximum_bitcast_fusion), channel_id=2, replica_groups=mesh['dp_0'=4,'dp_1'=4,'vocab_0'=4,'vocab_1'=2] {'vocab_0','vocab_1'}, dimensions={0}, use_global_device_ids=true | all-gather | bytes 13824 | tf_op jit(solution)/shard_map/all_gather | solution.py:145
  319.9 0.5 fusion.40
  320.5 2.8 copy.55
  (75 shorter events, 4.2 us)
Async XLA Ops:
  7.2 6.4 %copy-start = (bf16[128,8,1024]{2,1,0:T(8,128)(2,1)S(1)}, bf16[128,8,1024]{2,1,0:T(8,128)(2,1)}, u32[]{:S(2)}) copy-start(bf16[128,8,1024]{2,1,0:T(8,128)(2,1)} %param.11) | copy-start | bytes 6291460
  7.2 5.8 %copy-start.7 = (s32[128]{0:T(128)S(1)}, s32[128]{0:T(128)}, u32[]{:S(2)}) copy-start(s32[128]{0:T(128)} %param.17) | copy-start | bytes 1540
  7.2 5.8 %copy-start.3 = (s32[128,8]{0,1:T(8,128)S(1)}, s32[128,8]{0,1:T(8,128)}, u32[]{:S(2)}) copy-start(s32[128,8]{0,1:T(8,128)} %param.12) | copy-start | bytes 12292
  11.5 26.7 %collective-permute-start.1 = (bf16[512,3584]{1,0:T(8,128)(2,1)}, bf16[512,3584]{1,0:T(8,128)(2,1)}, u32[]{:S(2)}, u32[]{:S(2)}) collective-permute-start(bf16[512,3584]{1,0:T(8,128)(2,1)} %dynamic-slice_bitcast_fusion), channel_id=1, source_target_pairs={{0,1},{1,0},{2,3},{3,2},{4,5},{5,4},{6,7},{7,6},{8,9},{9,8},{10,11... | collective-permute-start | bytes 11010056 | tf_op jit(solution)/shard_map/ppermute | solution.py:34
  32.1 6.0 %collective-permute-start = (bf16[384,512]{1,0:T(8,128)(2,1)S(1)}, bf16[384,512]{1,0:T(8,128)(2,1)S(1)}, u32[]{:S(2)}, u32[]{:S(2)}) collective-permute-start(bf16[384,512]{1,0:T(8,128)(2,1)S(1)} %bitcast.57), channel_id=1, source_target_pairs={{0,1},{1,0},{2,3},{3,2},{4,5},{5,4},{6,7},{7,6},{8,9},{9,8},{10,11... | collective-permute-start | bytes 1179656 | tf_op jit(solution)/shard_map/ppermute | solution.py:34
  43.3 4.0 %copy-start.4 = (f32[128,8]{0,1:T(8,128)S(1)}, f32[128,8]{0,1:T(8,128)}, u32[]{:S(2)}) copy-start(f32[128,8]{0,1:T(8,128)} %param.13) | copy-start | bytes 12292
  43.3 41.4 %all-to-all-start.1 = ((bf16[16,24,3584]{2,1,0:T(8,128)(2,1)}), bf16[16,24,3584]{2,1,0:T(8,128)(2,1)S(1)}, u32[]{:S(2)}, u32[]{:S(2)}) async-start(bf16[16,24,3584]{2,1,0:T(8,128)(2,1)} %bitcast.56), calls=%async_computation.1 | async-start | bytes 5505024 | tf_op jit(solution)/shard_map/all_to_all | solution.py:77
  86.9 21.2 %copy-start.2 = (f32[7168]{0:T(1024)S(1)}, f32[7168]{0:T(1024)}, u32[]{:S(2)}) copy-start(f32[7168]{0:T(1024)} %param.15) | copy-start | bytes 86020
  86.9 16.2 %all-to-all-start.2 = ((bf16[4,32,3584]{2,1,0:T(8,128)(2,1)}), bf16[4,32,3584]{2,1,0:T(8,128)(2,1)S(1)}, u32[]{:S(2)}, u32[]{:S(2)}) async-start(bf16[4,32,3584]{2,1,0:T(8,128)(2,1)} %bitcast.17), calls=%async_computation.2 | async-start | bytes 1835008 | tf_op jit(solution)/shard_map/all_to_all | solution.py:90
  91.0 97.0 %all-gather.5.cloned.1.call-start = ((), (), s32[]{:S(2)}) async-start(), calls=%async_computation.5 | async-start | bytes 14794752 | tf_op jit(solution)/shard_map/all_gather | solution.py:135
  104.2 3.7 %collective-permute-start.2 = (bf16[16,3584]{1,0:T(8,128)(2,1)S(1)}, bf16[16,3584]{1,0:T(8,128)(2,1)S(1)}, u32[]{:S(2)}, u32[]{:S(2)}) collective-permute-start(bf16[16,3584]{1,0:T(8,128)(2,1)S(1)} %get-tuple-element.19), channel_id=1, source_target_pairs={{0,1},{1,0},{2,3},{3,2},{4,5},{5,4},{6,7},{7,6},{8,9},{9,8},{10,11... | collective-permute-start | bytes 344072 | tf_op jit(solution)/shard_map/ppermute | solution.py:34
  109.0 158.2 %all-gather.7.cloned.1.call-start = ((), (), s32[]{:S(2)}) async-start(), calls=%async_computation.6 | async-start | bytes 14794752 | tf_op jit(solution)/shard_map/all_gather | solution.py:135
  112.0 182.7 %all-to-all-start.3 = ((bf16[8,16,7168]{2,1,0:T(8,128)(2,1)}), bf16[8,16,7168]{2,1,0:T(8,128)(2,1)}, u32[]{:S(2)}, u32[]{:S(2)}) async-start(bf16[8,16,7168]{2,1,0:T(8,128)(2,1)} %broadcast_in_dim.25), calls=%async_computation.3 | async-start | bytes 3670016 | tf_op jit(solution)/shard_map/all_to_all | solution.py:123
  288.3 31.6 %copy-start.5 = (f32[128]{0:T(128)S(1)}, f32[128]{0:T(128)}, u32[]{:S(2)}) copy-start(f32[128]{0:T(128)} %param.19) | copy-start | bytes 1540
  288.3 31.6 %copy-start.6 = (f32[128]{0:T(128)S(1)}, f32[128]{0:T(128)}, u32[]{:S(2)}) copy-start(f32[128]{0:T(128)} %param.18) | copy-start | bytes 1540
  288.3 35.0 %copy-start.1 = (bf16[128,8,1024]{2,1,0:T(8,128)(2,1)S(1)}, bf16[128,8,1024]{2,1,0:T(8,128)(2,1)}, u32[]{:S(2)}) copy-start(bf16[128,8,1024]{2,1,0:T(8,128)(2,1)} %param.11) | copy-start | bytes 6291460
  294.7 12.2 %all-to-all-start.4 = ((f32[16,3,128]{2,1,0:T(4,128)}), f32[16,3,128]{2,1,0:T(4,128)S(1)}, u32[]{:S(2)}, u32[]{:S(2)}) async-start(f32[16,3,128]{2,1,0:T(4,128)} %copy.49), calls=%async_computation.4 | async-start | bytes 65536 | tf_op jit(solution)/shard_map/all_to_all | solution.py:143
Sparse Core Ops, SparseCore 0:
  109.1 78.8 all-gather.4
  191.0 76.1 all-gather.6
where the time goes:
time: 331 us; the launch traced here: 330 us
  waiting for transfers between devices  187 us (56%)
  matrix products  52.2 us (16%)
  blocking collectives  30.6 us (9%)
  starting transfers between devices  24.8 us (7%)
  between operations  14.4 us (4%)
  local copies, waits for them, and re-layouts  12.8 us (4%)
  other arithmetic  8.41 us (3%)
    all_gather x2, waiting for transfers between devices, per_device(): normed = lax.all_gather(piece, DP_VOCAB, axis=0, tiled=True)  130 us
    dot_general x7, matrix products, dot(): return jnp.dot(a, b, preferred_element_type=f32)  52.2 us
    all_to_all x1, waiting for transfers between devices, experts_stage(): back = lax.all_to_all(product.reshape(16, 24, cols), DP, 0, 0, tiled=True)  36.7 us
    all_to_all x1, blocking collectives, experts_stage(): received = lax.all_to_all(buffer, DP, 0, 0, tiled=True)  17.8 us
    all_gather x1, blocking collectives, per_device(): sent = lax.all_gather(group, VOCAB, axis=0)  12.8 us
    all_to_all x1, waiting for transfers between devices, experts_stage(): lax.all_to_all(partial.reshape(4, rows // 4, cols), X, 0, 0, tiled=True)  12 us
  transfers between devices with their start and end apart: 9, of which 6 were waited for; matrix products, arithmetic and copies ran while one was open for 17% of the time, Pallas kernels for 0%

commit v1 on v0

--- a/solution.py
+++ b/solution.py
@@ -132,7 +132,9 @@
     stats = []
     for c in range(2):
         piece = normed_sub[c * (sub // 2) : (c + 1) * (sub // 2)]
-        normed = lax.all_gather(piece, DP_VOCAB, axis=0, tiled=True)
+        normed = jnp.concatenate(
+            lax.all_to_all(jnp.stack([piece] * lax.axis_size(DP_VOCAB)), DP_VOCAB, 0, 0), axis=0
+        )
         logits = dot(normed, head_weight)
         peak = jnp.max(logits, axis=1)
         total = jnp.sum(jnp.exp(logits - peak[:, None]), axis=1)

time: 331 us -> 564 us (1.70)
  blocking collectives: 30.6 us -> 207 us
  waiting for transfers between devices: 187 us -> 232 us
  local copies, waits for them, and re-layouts: 12.8 us -> 26.2 us
  between operations: 14.4 us -> 1.05 us
  starting transfers between devices: 24.8 us -> 34.7 us
    all_to_all x0 -> x1, waiting for transfers between devices: none -> 176 us  [per_device(): lax.all_to_all(jnp.stack([piece] * lax.axis_size(DP_VOCAB)), DP_VOCAB, 0, 0)]
    all_to_all x0 -> x1, blocking collectives: none -> 175 us  [per_device(): lax.all_to_all(jnp.stack([piece] * lax.axis_size(DP_VOCAB)), DP_VOCAB, 0, 0)]
    all_gather x2 -> x0, waiting for transfers between devices: 130 us -> none  [per_device(): normed = lax.all_gather(piece, DP_VOCAB, axis=0, tiled=True)]
    another operation x0 -> x2, local copies, waits for them, and re-layouts: none -> 14.1 us  [per_device(): jnp.stack([piece] * lax.axis_size(DP_VOCAB))]
    all_to_all x0 -> x1, starting transfers between devices: none -> 9.05 us  [per_device(): lax.all_to_all(jnp.stack([piece] * lax.axis_size(DP_VOCAB)), DP_VOCAB, 0, 0)]
  transfers between devices with their start and end apart: 9 -> 8, of which waited for: 6 -> 5; matrix products, arithmetic and copies ran while one was open for 17% -> 10% of each run, Pallas kernels for 0% -> 0%
where the time goes in v1:
time: 564 us; the launch traced here: 563 us
  waiting for transfers between devices  232 us (41%)
  blocking collectives  207 us (37%)
  matrix products  53.8 us (10%)
  starting transfers between devices  34.7 us (6%)
  local copies, waits for them, and re-layouts  26.2 us (5%)
  other arithmetic  8.41 us (1%)
    all_to_all x1, waiting for transfers between devices, per_device(): lax.all_to_all(jnp.stack([piece] * lax.axis_size(DP_VOCAB)), DP_VOCAB, 0, 0)  176 us
    all_to_all x1, blocking collectives, per_device(): lax.all_to_all(jnp.stack([piece] * lax.axis_size(DP_VOCAB)), DP_VOCAB, 0, 0)  175 us
    dot_general x7, matrix products, dot(): return jnp.dot(a, b, preferred_element_type=f32)  53.8 us
    all_to_all x1, waiting for transfers between devices, experts_stage(): back = lax.all_to_all(product.reshape(16, 24, cols), DP, 0, 0, tiled=True)  36.8 us
    all_to_all x1, blocking collectives, experts_stage(): received = lax.all_to_all(buffer, DP, 0, 0, tiled=True)  17.8 us
    another operation x2, local copies, waits for them, and re-layouts, per_device(): jnp.stack([piece] * lax.axis_size(DP_VOCAB))  14.1 us
    all_gather x1, blocking collectives, per_device(): sent = lax.all_gather(group, VOCAB, axis=0)  13.8 us
    all_to_all x1, waiting for transfers between devices, experts_stage(): lax.all_to_all(partial.reshape(4, rows // 4, cols), X, 0, 0, tiled=True)  12 us
  transfers between devices with their start and end apart: 8, of which 5 were waited for; matrix products, arithmetic and copies ran while one was open for 10% of the time, Pallas kernels for 0%

profile of v1, /device:TPU:1, one launch (start us, length us, event | category | flops | bytes accessed | tf_op | source)
XLA Modules:
  0.0 563.3 jit_solution(16420926928310033634)
XLA Ops:
  0.7 4.3 dynamic-slice_bitcast_fusion
  4.9 1.4 collective-permute-start.1
  7.1 0.6 fusion.10
  7.7 17.8 %all_to_all.35 = bf16[16,32,512]{2,1,0:T(8,128)(2,1)S(1)} all-to-all(bf16[16,32,512]{2,1,0:T(8,128)(2,1)S(1)} %pad_maximum_fusion), channel_id=1, replica_groups=mesh['dp_0'=4,'dp_1'=4,'vocab_0'=4,'vocab_1'=2] {'dp_0','dp_1'}, dimensions={0} | all-to-all | bytes 1048576 | tf_op jit(solution)/shard_map/all_to_all | solution.py:69
  25.6 2.4 collective-permute-start
  28.0 3.6 fusion.5
  31.6 5.2 fusion.4
  36.8 4.6 all-to-all-start.1
  42.2 36.8 %all-to-all-done.1 = bf16[16,24,3584]{2,1,0:T(8,128)(2,1)} async-done(((bf16[16,24,3584]{2,1,0:T(8,128)(2,1)}), bf16[16,24,3584]{2,1,0:T(8,128)(2,1)}, u32[]{:S(2)}, u32[]{:S(2)}) %all-to-all-start.1) | async-done | bytes 2752544 | tf_op jit(solution)/shard_map/all_to_all | solution.py:77
  78.9 2.9 fusion.17
  81.8 1.1 fusion.8
  82.9 4.1 all-to-all-start.2
  87.1 12.0 %all-to-all-done.2 = bf16[4,32,3584]{2,1,0:T(8,128)(2,1)S(1)} async-done(((bf16[4,32,3584]{2,1,0:T(8,128)(2,1)}), bf16[4,32,3584]{2,1,0:T(8,128)(2,1)S(1)}, u32[]{:S(2)}, u32[]{:S(2)}) %all-to-all-start.2) | async-done | bytes 917536 | tf_op jit(solution)/shard_map/all_to_all | solution.py:90
  99.2 1.0 add_convert_fusion
  100.3 2.7 collective-permute-start.2
  102.9 1.0 collective-permute-done.2
  104.3 7.0 %stack.28 = bf16[128,8,7168]{2,1,0:T(8,128)(2,1)} broadcast(bf16[8,7168]{1,0:T(8,128)(2,1)S(1)} %get-tuple-element.17), dimensions={1,2} | broadcast | bytes 14794752 | tf_op jit(solution)/shard_map/stack | solution.py:136
  111.3 175.2 %all_to_all.36 = bf16[128,8,7168]{2,1,0:T(8,128)(2,1)} all-to-all(bf16[128,8,7168]{2,1,0:T(8,128)(2,1)} %stack.28), channel_id=1, replica_groups=mesh['dp_0'=4,'dp_1'=4,'vocab_0'=4,'vocab_1'=2] {'dp_0','dp_1','vocab_0'..., dimensions={0} | all-to-all | bytes 29360128 | tf_op jit(solution)/shard_map/all_to_all | solution.py:136
  286.6 7.0 %stack.33 = bf16[128,8,7168]{2,1,0:T(8,128)(2,1)} broadcast(bf16[8,7168]{1,0:T(8,128)(2,1)S(1)} %get-tuple-element.18), dimensions={1,2} | broadcast | bytes 14794752 | tf_op jit(solution)/shard_map/stack | solution.py:136
  293.6 9.0 %all-to-all-start.5 = ((bf16[128,8,7168]{2,1,0:T(8,128)(2,1)}), bf16[128,8,7168]{2,1,0:T(8,128)(2,1)}, u32[]{:S(2)}, u32[]{:S(2)}) async-start(bf16[128,8,7168]{2,1,0:T(8,128)(2,1)} %stack.33), calls=%async_computation.5 | async-start | bytes 29360128 | tf_op jit(solution)/shard_map/all_to_all | solution.py:136
  303.6 20.8 %fusion.48 = (f32[1024]{0:T(1024)S(1)}, f32[1024,896]{0,1:T(8,128)}) fusion(bf16[7168,896]{1,0:T(8,128)(2,1)} %param.16, bf16[128,8,7168]{2,1,0:T(8,128)(2,1)} %all_to_all.36), kind=kOutput, calls=%fused_computation.110 | convolution fusion | flops 13154253824 | bytes 31199232 | tf_op jit(solution)/shard_map/dot_general | solution.py:30
  324.3 176.1 %all-to-all-done.5 = bf16[128,8,7168]{2,1,0:T(8,128)(2,1)} async-done(((bf16[128,8,7168]{2,1,0:T(8,128)(2,1)}), bf16[128,8,7168]{2,1,0:T(8,128)(2,1)}, u32[]{:S(2)}, u32[]{:S(2)}) %all-to-all-start.5) | async-done | bytes 14680096 | tf_op jit(solution)/shard_map/all_to_all | solution.py:136
  500.4 1.4 broadcast_in_dim.25
  501.8 7.0 %all-to-all-start.3 = ((bf16[8,16,7168]{2,1,0:T(8,128)(2,1)}), bf16[8,16,7168]{2,1,0:T(8,128)(2,1)}, u32[]{:S(2)}, u32[]{:S(2)}) async-start(bf16[8,16,7168]{2,1,0:T(8,128)(2,1)} %broadcast_in_dim.25), calls=%async_computation.3 | async-start | bytes 3670016 | tf_op jit(solution)/shard_map/all_to_all | solution.py:123
  508.8 20.6 %fusion.49 = (f32[1024]{0:T(1024)S(1)}, f32[1024,896]{0,1:T(8,128)}) fusion(bf16[7168,896]{1,0:T(8,128)(2,1)} %param.16, bf16[128,8,7168]{2,1,0:T(8,128)(2,1)} %all-to-all-done.5), kind=kOutput, calls=%fused_computation.111 | convolution fusion | flops 13154253824 | bytes 31199232 | tf_op jit(solution)/shard_map/dot_general | solution.py:30
  529.6 4.3 exponential_reduce_fusion.1
  535.4 0.6 copy.49
  536.0 3.5 all-to-all-start.6
  539.5 6.4 %all-to-all-done.6 = f32[16,3,128]{2,1,0:T(4,128)S(1)} async-done(((f32[16,3,128]{2,1,0:T(4,128)}), f32[16,3,128]{2,1,0:T(4,128)S(1)}, u32[]{:S(2)}, u32[]{:S(2)}) %all-to-all-start.6) | async-done | bytes 24608 | tf_op jit(solution)/shard_map/all_to_all | solution.py:145
  546.1 13.8 %all-gather.1 = f32[8,3,128]{2,1,0:T(4,128)S(1)} all-gather(f32[1,3,128]{2,1,0:T(4,128)S(1)} %maximum_bitcast_fusion), channel_id=2, replica_groups=mesh['dp_0'=4,'dp_1'=4,'vocab_0'=4,'vocab_1'=2] {'vocab_0','vocab_1'}, dimensions={0}, use_global_device_ids=true | all-gather | bytes 13824 | tf_op jit(solution)/shard_map/all_gather | solution.py:147
  559.9 0.5 fusion.44
  560.5 2.8 copy.55
  (74 shorter events, 4.7 us)
Async XLA Ops:
  0.6 6.4 %copy-start = (bf16[128,8,1024]{2,1,0:T(8,128)(2,1)S(1)}, bf16[128,8,1024]{2,1,0:T(8,128)(2,1)}, u32[]{:S(2)}) copy-start(bf16[128,8,1024]{2,1,0:T(8,128)(2,1)} %param.11) | copy-start | bytes 6291460
  0.7 5.8 %copy-start.3 = (s32[128,8]{0,1:T(8,128)S(1)}, s32[128,8]{0,1:T(8,128)}, u32[]{:S(2)}) copy-start(s32[128,8]{0,1:T(8,128)} %param.12) | copy-start | bytes 12292
  0.7 6.0 %copy-start.7 = (s32[128]{0:T(128)S(1)}, s32[128]{0:T(128)}, u32[]{:S(2)}) copy-start(s32[128]{0:T(128)} %param.17) | copy-start | bytes 1540
  4.9 26.7 %collective-permute-start.1 = (bf16[512,3584]{1,0:T(8,128)(2,1)}, bf16[512,3584]{1,0:T(8,128)(2,1)}, u32[]{:S(2)}, u32[]{:S(2)}) collective-permute-start(bf16[512,3584]{1,0:T(8,128)(2,1)} %dynamic-slice_bitcast_fusion), channel_id=1, source_target_pairs={{0,1},{1,0},{2,3},{3,2},{4,5},{5,4},{6,7},{7,6},{8,9},{9,8},{10,11... | collective-permute-start | bytes 11010056 | tf_op jit(solution)/shard_map/ppermute | solution.py:34
  25.6 6.0 %collective-permute-start = (bf16[384,512]{1,0:T(8,128)(2,1)S(1)}, bf16[384,512]{1,0:T(8,128)(2,1)S(1)}, u32[]{:S(2)}, u32[]{:S(2)}) collective-permute-start(bf16[384,512]{1,0:T(8,128)(2,1)S(1)} %bitcast.64), channel_id=1, source_target_pairs={{0,1},{1,0},{2,3},{3,2},{4,5},{5,4},{6,7},{7,6},{8,9},{9,8},{10,11... | collective-permute-start | bytes 1179656 | tf_op jit(solution)/shard_map/ppermute | solution.py:34
  36.8 4.7 copy-start.4
  36.8 42.2 %all-to-all-start.1 = ((bf16[16,24,3584]{2,1,0:T(8,128)(2,1)}), bf16[16,24,3584]{2,1,0:T(8,128)(2,1)}, u32[]{:S(2)}, u32[]{:S(2)}) async-start(bf16[16,24,3584]{2,1,0:T(8,128)(2,1)} %bitcast.63), calls=%async_computation.1 | async-start | bytes 5505024 | tf_op jit(solution)/shard_map/all_to_all | solution.py:77
  82.9 21.2 %copy-start.2 = (f32[7168]{0:T(1024)S(1)}, f32[7168]{0:T(1024)}, u32[]{:S(2)}) copy-start(f32[7168]{0:T(1024)} %param.15) | copy-start | bytes 86020
  82.9 16.2 %all-to-all-start.2 = ((bf16[4,32,3584]{2,1,0:T(8,128)(2,1)}), bf16[4,32,3584]{2,1,0:T(8,128)(2,1)S(1)}, u32[]{:S(2)}, u32[]{:S(2)}) async-start(bf16[4,32,3584]{2,1,0:T(8,128)(2,1)} %bitcast.17), calls=%async_computation.2 | async-start | bytes 1835008 | tf_op jit(solution)/shard_map/all_to_all | solution.py:90
  100.3 3.7 collective-permute-start.2
  293.6 206.8 %all-to-all-start.5 = ((bf16[128,8,7168]{2,1,0:T(8,128)(2,1)}), bf16[128,8,7168]{2,1,0:T(8,128)(2,1)}, u32[]{:S(2)}, u32[]{:S(2)}) async-start(bf16[128,8,7168]{2,1,0:T(8,128)(2,1)} %stack.33), calls=%async_computation.5 | async-start | bytes 29360128 | tf_op jit(solution)/shard_map/all_to_all | solution.py:136
  501.8 34.2 %all-to-all-start.3 = ((bf16[8,16,7168]{2,1,0:T(8,128)(2,1)}), bf16[8,16,7168]{2,1,0:T(8,128)(2,1)}, u32[]{:S(2)}, u32[]{:S(2)}) async-start(bf16[8,16,7168]{2,1,0:T(8,128)(2,1)} %broadcast_in_dim.25), calls=%async_computation.3 | async-start | bytes 3670016 | tf_op jit(solution)/shard_map/all_to_all | solution.py:123
  529.6 30.3 %copy-start.5 = (f32[128]{0:T(128)S(1)}, f32[128]{0:T(128)}, u32[]{:S(2)}) copy-start(f32[128]{0:T(128)} %param.19) | copy-start | bytes 1540
  529.6 30.3 %copy-start.6 = (f32[128]{0:T(128)S(1)}, f32[128]{0:T(128)}, u32[]{:S(2)}) copy-start(f32[128]{0:T(128)} %param.18) | copy-start | bytes 1540
  529.6 33.7 %copy-start.1 = (bf16[128,8,1024]{2,1,0:T(8,128)(2,1)S(1)}, bf16[128,8,1024]{2,1,0:T(8,128)(2,1)}, u32[]{:S(2)}) copy-start(bf16[128,8,1024]{2,1,0:T(8,128)(2,1)} %param.11) | copy-start | bytes 6291460
  536.0 9.9 %all-to-all-start.6 = ((f32[16,3,128]{2,1,0:T(4,128)}), f32[16,3,128]{2,1,0:T(4,128)S(1)}, u32[]{:S(2)}, u32[]{:S(2)}) async-start(f32[16,3,128]{2,1,0:T(4,128)} %copy.49), calls=%async_computation.6 | async-start | bytes 65536 | tf_op jit(solution)/shard_map/all_to_all | solution.py:145
